TPU v7x, 32 devices: a whole 2x2x4 slice. The times are simulated.
32 devices in a mesh: north: 4 (over x, core), east: 8 (over z, y).
Axes of the slice: x: 2, y: 2, z: 4, core: 2. Of those that a mesh axis runs over, the one named last changes fastest.
Arguments:
- left_factor: bfloat16 [4096, 2048], P('north', 'east'), may hold values from -6 to 6
- right_factor: bfloat16 [2048, 4096], P('north', 'east'), may hold values from -0.125 to 0.125
Outputs:
- updated: float32 [4096, 4096], P('north', 'east')
All inputs are finite; a program needn't handle non-finite values.
Results may differ from a plain program's by a relative error of at most 0.0003.
Values may be sent and summed in bfloat16 or wider, within the bound.
A program may use at most 128 MiB of HBM per device.

v0:
```python
import jax
import jax.numpy as jnp
from jax import lax
from jax.sharding import PartitionSpec as P


def over_all(piece, axis, dim, lap, start):

    def gathered(part):
        return lax.all_gather(part, axis, axis=dim, tiled=True)

    return lap(start, jax.tree.map(gathered, piece), jnp.int32(0))


def absorb_panel(carry, left_panel, right_panel):
    return carry + jnp.dot(left_panel, right_panel, preferred_element_type=jnp.float32)


def shards(left_factor, right_factor):
    begin = jnp.zeros((left_factor.shape[0], right_factor.shape[1]), jnp.float32)
    left_line = lax.all_gather(left_factor, "east", axis=1, tiled=True)

    def take_rows(carry, piece, start):
        left_piece = lax.dynamic_slice_in_dim(left_line, start, piece.shape[0], axis=1)
        return absorb_panel(carry, left_piece, piece)

    total = over_all(right_factor, "north", 0, take_rows, begin)
    updated = total
    row_power = lax.psum(jnp.sum(updated * updated, axis=1), "east")
    updated = (
        updated * lax.rsqrt(row_power / (updated.shape[1] * lax.axis_size("east")) + 1e-06)[:, None]
    )
    return updated


def solution(mesh):
    placed = (P("north", "east"), P("north", "east"))
    return jax.shard_map(
        shards, mesh=mesh, in_specs=placed, out_specs=P("north", "east"), check_vma=False
    )
```

profile of v0, /device:TPU:0, one launch (start us, length us, event | category | flops | bytes accessed | tf_op | source)
XLA Modules:
  0.0 146.5 jit_solution(11622587532451686640)
XLA Ops:
  6.5 0.0 all-gather.5.cloned.1.call-start
  6.5 0.7 all-gather.5.cloned.1.call-update
  7.3 0.0 all-gather.3.cloned.1.call-start
  7.3 0.7 all-gather.3.cloned.1.call-update
  8.0 26.2 %all-gather.5.cloned.1.call-done = bf16[2048,512]{1,0:T(8,128)(2,1)} async-done(((bf16[512,512]{1,0:T(8,128)(2,1)}), bf16[2048,512]{1,0:T(8,128)(2,1)}) %all-gather.5.cloned.1.call-update) | async-done | bytes 2097168 | tf_op jit(solution)/shard_map/all_gather | solution.py:10
  34.2 76.7 %all-gather.3.cloned.1.call-done = bf16[1024,2048]{1,0:T(8,128)(2,1)} async-done(((bf16[1024,256]{1,0:T(8,128)(2,1)}), bf16[1024,2048]{1,0:T(8,128)(2,1)}) %all-gather.3.cloned.1.call-update) | async-done | bytes 4194320 | tf_op jit(solution)/shard_map/all_gather | solution.py:21
  110.9 6.6 %multiply_reduce_fusion = (f32[1024]{0:T(1024)S(1)}, f32[1024,512]{0,1:T(8,128)}) fusion(bf16[1024,2048]{1,0:T(8,128)(2,1)} %all-gather.3.cloned.1.call-done, bf16[2048,512]{1,0:T(8,128)(2,1)} %all-gather.5.cloned.1.call-done), kind=kOutput, calls=%fused_computation | convolution fusion | flops 2148531200 | bytes 8392704 | tf_op jit(solution)/shard_map/dot_general | solution.py:16
  117.5 18.6 %psum.7 = f32[1024]{0:T(1024)S(1)} all-reduce(f32[1024]{0:T(1024)S(1)} %get-tuple-element.5), channel_id=1, replica_groups=mesh['north'=4,'east'=8] {'east'}, use_global_device_ids=true, to_apply=%region_1.0 | all-reduce | flops 1024 | bytes 8192 | tf_op jit(solution)/shard_map/psum | solution.py:29
  136.0 1.8 %broadcast_multiply_fusion = f32[1024,512]{0,1:T(8,128)S(1)} fusion(f32[1024,512]{0,1:T(8,128)} %get-tuple-element.6, f32[1024]{0:T(1024)S(1)} %add_rsqrt_fusion), kind=kLoop, calls=%fused_computation.1 | loop fusion | flops 524288 | bytes 4198400 | tf_op jit(solution)/shard_map/mul | solution.py:31
  137.9 1.8 %copy.3 = f32[1024,512]{1,0:T(8,128)} copy(f32[1024,512]{0,1:T(8,128)S(1)} %broadcast_multiply_fusion) | data formatting | bytes 4194304 | tf_op jit(solution)/shard_map/mul | solution.py:31
  (1 shorter events, 0.0 us)
Async XLA Ops:
  6.5 27.7 %all-gather.5.cloned.1.call-start = ((), (), s32[]{:S(2)}) async-start(), calls=%async_computation.1 | async-start | bytes 2621440 | tf_op jit(solution)/shard_map/all_gather | solution.py:10
  7.3 103.7 %all-gather.3.cloned.1.call-start = ((), (), s32[]{:S(2)}) async-start(), calls=%async_computation | async-start | bytes 4718592 | tf_op jit(solution)/shard_map/all_gather | solution.py:21
Sparse Core Ops, SparseCore 0:
  8.9 25.2 all-gather.4
  36.2 74.6 all-gather.2
where the time goes:
time: 147 us
  waiting for transfers between devices  104 us (71%)
  blocking collectives  18.6 us (13%)
  between operations  13.4 us (9%)
  matrix products  6.56 us (4%)
  other arithmetic  1.82 us (1%)
  local copies, waits for them, and re-layouts  1.81 us (1%)
    all_gather x1, waiting for transfers between devices, shards(): left_line = lax.all_gather(left_factor, 'east', axis=1, tiled=True)  76.7 us
    all_gather x1, waiting for transfers between devices, gathered(): return lax.all_gather(part, axis, axis=dim, tiled=True)  26.2 us
    psum x1, blocking collectives, shards(): row_power = lax.psum(jnp.sum(updated * updated, axis=1), 'east')  18.6 us
    dot_general x1, matrix products, absorb_panel(): jnp.dot(left_panel, right_panel, preferred_element_type=jnp.float32)  6.56 us
  transfers between devices with their start and end apart: 2, of which 2 were waited for; matrix products, arithmetic and copies ran while one was open for 0% of the time, Pallas kernels for 0%

commit v1 on v0

--- a/solution.py
+++ b/solution.py
@@ -1,7 +1,16 @@
+import functools
 import jax
 import jax.numpy as jnp
 from jax import lax
 from jax.sharding import PartitionSpec as P
+from jax.lax import all_gather
+
+
+def edge_refer(array_in, device_axis):
+    return jnp.sum(all_gather(array_in, device_axis), 0)
+
+
+orders_point = functools.partial(edge_refer, device_axis="east")
 
 
 def over_all(piece, axis, dim, lap, start):
@@ -26,7 +35,7 @@
 
     total = over_all(right_factor, "north", 0, take_rows, begin)
     updated = total
-    row_power = lax.psum(jnp.sum(updated * updated, axis=1), "east")
+    row_power = orders_point(jnp.sum(updated * updated, axis=1))
     updated = (
         updated * lax.rsqrt(row_power / (updated.shape[1] * lax.axis_size("east")) + 1e-06)[:, None]
     )

time: 147 us -> 159 us (1.082)
  blocking collectives: 18.6 us -> 30.6 us
    all_gather x0 -> x1, blocking collectives: none -> 30.6 us  [edge_refer(): return jnp.sum(all_gather(array_in, device_axis), 0)]
    psum x1 -> x0, blocking collectives: 18.6 us -> none  [shards(): row_power = lax.psum(jnp.sum(updated * updated, axis=1), 'east')]
where the time goes in v1:
time: 159 us
  waiting for transfers between devices  104 us (65%)
  blocking collectives  30.6 us (19%)
  between operations  13.4 us (8%)
  matrix products  6.56 us (4%)
  local copies, waits for them, and re-layouts  1.83 us (1%)
  other arithmetic  1.83 us (1%)
    all_gather x1, waiting for transfers between devices, shards(): left_line = lax.all_gather(left_factor, 'east', axis=1, tiled=True)  76.7 us
    all_gather x1, blocking collectives, edge_refer(): return jnp.sum(all_gather(array_in, device_axis), 0)  30.6 us
    all_gather x1, waiting for transfers between devices, gathered(): return lax.all_gather(part, axis, axis=dim, tiled=True)  26.2 us
    dot_general x1, matrix products, absorb_panel(): jnp.dot(left_panel, right_panel, preferred_element_type=jnp.float32)  6.56 us
  transfers between devices with their start and end apart: 2, of which 2 were waited for; matrix products, arithmetic and copies ran while one was open for 0% of the time, Pallas kernels for 0%

profile of v1, /device:TPU:0, one launch (start us, length us, event | category | flops | bytes accessed | tf_op | source)
XLA Modules:
  0.0 158.6 jit_solution(6514375785777202662)
XLA Ops:
  6.5 0.0 all-gather.6.cloned.1.call-start
  6.5 0.7 all-gather.6.cloned.1.call-update
  7.3 0.0 all-gather.4.cloned.1.call-start
  7.3 0.7 all-gather.4.cloned.1.call-update
  8.0 26.2 %all-gather.6.cloned.1.call-done = bf16[2048,512]{1,0:T(8,128)(2,1)} async-done(((bf16[512,512]{1,0:T(8,128)(2,1)}), bf16[2048,512]{1,0:T(8,128)(2,1)}) %all-gather.6.cloned.1.call-update) | async-done | bytes 2097168 | tf_op jit(solution)/shard_map/all_gather | solution.py:19
  34.2 76.7 %all-gather.4.cloned.1.call-done = bf16[1024,2048]{1,0:T(8,128)(2,1)} async-done(((bf16[1024,256]{1,0:T(8,128)(2,1)}), bf16[1024,2048]{1,0:T(8,128)(2,1)}) %all-gather.4.cloned.1.call-update) | async-done | bytes 4194320 | tf_op jit(solution)/shard_map/all_gather | solution.py:30
  110.9 6.6 %multiply_reduce_fusion = (f32[1024]{0:T(1024)S(1)}, f32[1024,512]{0,1:T(8,128)}) fusion(bf16[1024,2048]{1,0:T(8,128)(2,1)} %all-gather.4.cloned.1.call-done, bf16[2048,512]{1,0:T(8,128)(2,1)} %all-gather.6.cloned.1.call-done), kind=kOutput, calls=%fused_computation | convolution fusion | flops 2148531200 | bytes 8392704 | tf_op jit(solution)/shard_map/dot_general | solution.py:25
  117.5 30.6 %all-gather = f32[8192]{0:T(1024)S(1)} all-gather(f32[1024]{0:T(1024)S(1)} %get-tuple-element.5), channel_id=2, replica_groups=mesh['north'=4,'east'=8] {'east'}, dimensions={0}, use_global_device_ids=true | all-gather | bytes 36864 | tf_op jit(solution)/shard_map/all_gather | solution.py:10
  148.1 1.8 %broadcast_multiply_fusion = f32[1024,512]{0,1:T(8,128)S(1)} fusion(f32[1024,512]{0,1:T(8,128)} %get-tuple-element.6, f32[1024]{0:T(1024)S(1)} %add_rsqrt_fusion), kind=kLoop, calls=%fused_computation.1 | loop fusion | flops 524288 | bytes 4198400 | tf_op jit(solution)/shard_map/mul | solution.py:40
  149.9 1.8 %copy.5 = f32[1024,512]{1,0:T(8,128)} copy(f32[1024,512]{0,1:T(8,128)S(1)} %broadcast_multiply_fusion) | data formatting | bytes 4194304 | tf_op jit(solution)/shard_map/mul | solution.py:40
  (3 shorter events, 0.0 us)
Async XLA Ops:
  6.5 27.7 %all-gather.6.cloned.1.call-start = ((), (), s32[]{:S(2)}) async-start(), calls=%async_computation.1 | async-start | bytes 2621440 | tf_op jit(solution)/shard_map/all_gather | solution.py:19
  7.3 103.7 %all-gather.4.cloned.1.call-start = ((), (), s32[]{:S(2)}) async-start(), calls=%async_computation | async-start | bytes 4718592 | tf_op jit(solution)/shard_map/all_gather | solution.py:30
Sparse Core Ops, SparseCore 0:
  8.9 25.2 all-gather.5
  36.2 74.6 all-gather.3
